TPU v7x, 32 devices: a whole 2x2x4 slice. The times are simulated.
32 devices in a mesh: pb: 4 (over x, core), pq: 8 (over z, y).
Axes of the slice: x: 2, y: 2, z: 4, core: 2. Of those that a mesh axis runs over, the one named last changes fastest.
Arguments:
- chol_vv: bfloat16 [176, 1792, 1792], P('pb', 'pq'), may hold values from -6 to 6
- chol_ov: bfloat16 [176, 256, 1792], P('pb', 'pq'), may hold values from -6 to 6
- chol_oo: bfloat16 [176, 256, 256], P('pb', 'pq'), may hold values from -6 to 6
- chol_vo: bfloat16 [176, 256, 1792], P('pb', None, 'pq'), may hold values from -6 to 6
- amplitudes: bfloat16 [256, 1792], P(None, 'pq'), may hold values from -0.125 to 0.125
Outputs:
- dressed: bfloat16 [176, 256, 1792], P('pb', 'pq')
- fock_ov: float32 [256, 1792], P('pq')
All inputs are finite; a program needn't handle non-finite values.
Results may differ from a plain program's by a relative error of at most 0.0081.
Values may be sent and summed in bfloat16 or wider, within the bound.
A program may use at most 128 MiB of HBM per device.

v0:
```python
import functools

import jax
import jax.numpy as jnp
from jax import lax
from jax.experimental import pallas as pl
from jax.experimental.pallas import tpu as pltpu
from jax.sharding import PartitionSpec as P

MESH = pl.DeviceIdType.MESH


def per_device(chol_vv, chol_ov, chol_oo, chol_vo, amplitudes):
    batch = chol_vv.shape[0]
    occ_rows = chol_ov.shape[1]
    whole_amps = lax.all_gather(amplitudes, "pq", axis=1, tiled=True)
    lprime = (
        chol_oo.astype(jnp.float32)
        + jnp.einsum("qjb,ib->qji", chol_ov, whole_amps, preferred_element_type=jnp.float32)
    ).astype(jnp.bfloat16)
    direct = jnp.einsum("qab,ib->qia", chol_vv, whole_amps, preferred_element_type=jnp.float32)
    partial_sum = chol_vo.astype(jnp.float32) + direct
    occupied = jnp.einsum(
        "qji,ja->qia",
        lax.all_gather(lprime, "pq", axis=1, tiled=True),
        amplitudes,
        preferred_element_type=jnp.float32,
    )
    local_dressed = (partial_sum - occupied).astype(jnp.bfloat16)
    dressed = lax.all_to_all(local_dressed, "pq", split_axis=1, concat_axis=2, tiled=True)
    row_start = lax.axis_index("pq") * occ_rows
    own_amps = lax.dynamic_slice_in_dim(whole_amps, row_start, occ_rows, 0)
    local_coulomb = 2.0 * jnp.einsum(
        "qia,ia->q", dressed, own_amps, preferred_element_type=jnp.float32
    )
    coulomb = lax.psum(local_coulomb, "pq")
    local_fock = jnp.sum(coulomb[:, None, None] * dressed.astype(jnp.float32), axis=0)
    fock_ov = lax.psum(local_fock, "pb") / (batch * lax.axis_size("pb"))
    return (dressed, fock_ov)


def kernel(
    n, n_pb, group,
    vv_hbm, ov_hbm, oo_hbm, vo_hbm, amps_ref,
    dressed, fock_ref,
    vv_buf, ov_buf, oo_buf, vo_buf, amps_t, amps, tiled, gram,
    sent, got, coul_sent, coul_got, fock_sent, fock_got,
    load_sem, own_sem, gather_send, gather_recv, send_sem, recv_sem,
    coul_send, coul_recv, fock_send, fock_recv,
):
    me = lax.axis_index("pq")
    mine = lax.axis_index("pb")
    batch, virt, whole_virt = vv_hbm.shape
    rows, occ = ov_hbm.shape[1], oo_hbm.shape[2]
    steps = batch // group
    wide, deep = group * virt, group * rows
    peers = [lax.rem(me + d, n) for d in range(1, n)]
    core, place = lax.rem(mine, 2), mine // 2
    mate, across = mine + 1 - 2 * core, lax.rem(mine + 2, 4)
    partners = [mate, across]

    def loads(step, slot):
        part = pl.ds(step * group, group)
        pairs = ((vv_hbm, vv_buf), (ov_hbm, ov_buf), (oo_hbm, oo_buf), (vo_hbm, vo_buf))
        return [
            pltpu.make_async_copy(src.at[part], dst.at[slot], load_sem.at[slot, k])
            for k, (src, dst) in enumerate(pairs)
        ]

    for copy in loads(0, 0):
        copy.start()

    barrier = pltpu.get_barrier_semaphore()
    for peer in peers:
        pl.semaphore_signal(barrier, inc=1, device_id={"pq": peer}, device_id_type=MESH)
    for partner in partners:
        pl.semaphore_signal(barrier, inc=1, device_id={"pb": partner}, device_id_type=MESH)
    pl.semaphore_wait(barrier, len(peers) + len(partners))

    def remote(src, dst, send, recv, where):
        return pltpu.make_async_remote_copy(
            src_ref=src, dst_ref=dst, send_sem=send, recv_sem=recv,
            device_id=where, device_id_type=MESH,
        )

    half_virt, half_occ = virt // 2, occ // 2
    own_columns = pl.ds(pl.multiple_of(core * half_occ, 128), half_occ)

    def quarter(owner):
        first = pl.multiple_of(owner * virt + place * half_virt, 16)
        return amps_t.at[pl.ds(first, half_virt), own_columns]

    own_quarter = amps_ref.at[pl.ds(pl.multiple_of(place * half_virt, 16), half_virt), own_columns]
    gathers = [
        remote(own_quarter, quarter(me), gather_send.at[0, d], gather_recv.at[0, d], {"pq": peer})
        for d, peer in enumerate(peers)
    ]
    for copy in gathers:
        copy.start()
    own_block = pl.ds(pl.multiple_of(me * virt, 16), virt)
    own = pltpu.make_async_copy(amps_ref, amps_t.at[own_block], own_sem)
    own.start()
    own.wait()
    owners = [lax.rem(me + n - 1 - d, n) for d in range(n - 1)]
    crossing = [
        remote(quarter(owner), quarter(owner), gather_send.at[1, d], gather_recv.at[1, d], {"pb": across})
        for d, owner in enumerate(owners)
    ]
    swaps = []
    for d, owner in enumerate(owners):
        block = pl.ds(pl.multiple_of(owner * virt, 16), virt)
        half = amps_t.at[block, own_columns]
        swaps.append(remote(half, half, gather_send.at[2, d], gather_recv.at[2, d], {"pb": mate}))
    for d in range(n - 1):
        gathers[d].wait_recv()
        crossing[d].start()
    for d in range(n - 1):
        crossing[d].wait_recv()
        swaps[d].start()
    for d in range(n - 1):
        swaps[d].wait_recv()
    for copy in gathers + crossing + swaps:
        copy.wait_send()

    def exchange(step, d):
        return remote(
            sent.at[step, pl.ds(pl.multiple_of(peers[d] * rows, 16), rows)],
            got.at[step, me],
            send_sem.at[step, d], recv_sem.at[step, d], {"pq": peers[d]},
        )

    early = min(steps, 5)

    def form(slot):
        vv = vv_buf[slot].reshape(wide, whole_virt)
        direct = jnp.dot(vv, amps_t[...], preferred_element_type=jnp.float32)
        direct = direct + vo_buf[slot].reshape(wide, occ).astype(jnp.float32)
        ov = ov_buf[slot].reshape(deep, whole_virt)
        lprime = jnp.dot(ov, amps_t[...], preferred_element_type=jnp.float32)
        lprime = lprime + oo_buf[slot].reshape(deep, occ).astype(jnp.float32)
        return direct, lprime

    def put(step, direct, lprime):
        sent[step, :, 0:wide] = direct.T.astype(jnp.bfloat16)
        sent[step, :, wide:wide + deep] = lprime.T.astype(jnp.bfloat16)
        got[step, me] = sent[step, pl.ds(pl.multiple_of(me * rows, 16), rows), :]

    def send(step, carry):
        for d in range(n - 1):
            exchange(step, d).start()
        return carry

    for copy in loads(0, 0):
        copy.wait()
    put(0, *form(0))
    send(0, 0)

    for s in range(n):
        block = amps_t[s * virt:(s + 1) * virt, :]
        amps_t_f32 = block.astype(jnp.float32)
        tiled[:, s * virt:(s + 1) * virt] = amps_t_f32.T
    for s in range(n):
        part = tiled[s * rows:(s + 1) * rows, :].astype(jnp.bfloat16)
        for q in range(group):
            amps[s * deep + q * rows:s * deep + (q + 1) * rows, :] = part
    own_rows = amps[pl.ds(pl.multiple_of(me * deep, 128), rows), :]
    gram[...] = jnp.dot(own_rows, amps_t[...], preferred_element_type=jnp.float32)
    coul_sent[...] = jnp.zeros_like(coul_sent)

    def produce(step, carry):
        slot = lax.rem(step, 2)

        @pl.when(step + 1 < steps)
        def _():
            for copy in loads(step + 1, 1 - slot):
                copy.start()

        @pl.when(step > 0)
        def _():
            for copy in loads(step, slot):
                copy.wait()

        direct, lprime = form(slot)

        @pl.when(step > 0)
        def _():
            put(step, direct, lprime)

        own_amps = amps_ref[...].astype(jnp.float32)
        at_row = lax.broadcasted_iota(jnp.int32, coul_sent.shape, 0) == step
        lane = lax.broadcasted_iota(jnp.int32, coul_sent.shape, 1)
        held = coul_sent[...]
        for q in range(group):
            from_direct = direct[q * virt:(q + 1) * virt] * own_amps
            from_occ = lprime[q * rows:(q + 1) * rows] * gram[...]
            value = jnp.sum(from_direct) - jnp.sum(from_occ)
            held = jnp.where(at_row & (lane == q), value, held)
        coul_sent[...] = held

        @pl.when((step > 0) & (step < early))
        def _():
            send(step, 0)

        return carry

    lax.fori_loop(0, steps, produce, 0)

    coulombs = [
        remote(coul_sent, coul_got.at[d], coul_send.at[d], coul_recv.at[d], {"pq": peer})
        for d, peer in enumerate(peers)
    ]
    for copy in coulombs:
        copy.start()

    lax.fori_loop(early, steps, send, 0)

    for copy in coulombs:
        copy.wait()
    coulomb = coul_sent[...]
    for d in range(n - 1):
        coulomb = coulomb + coul_got[d]
    coul_sent[...] = coulomb
    fock_ref[...] = jnp.zeros_like(fock_ref)

    def consume(step, carry):
        for d in range(n - 1):
            exchange(step, d).wait()
        lane_q = lax.broadcasted_iota(jnp.int32, (rows, deep), 1) // rows
        columns = []
        for s in range(n):
            piece = got[step, s, :, wide:wide + deep]
            columns.append(jnp.concatenate(
                [jnp.where(lane_q == q, piece, jnp.zeros_like(piece)) for q in range(group)], axis=0
            ))
        occupied = jnp.dot(
            jnp.concatenate(columns, axis=1), amps[...], preferred_element_type=jnp.float32
        )
        weights = coul_sent[...]
        at_row = lax.broadcasted_iota(jnp.int32, weights.shape, 0) == step
        lane = lax.broadcasted_iota(jnp.int32, weights.shape, 1)
        total = fock_ref[...]
        for q in range(group):
            partial_sum = jnp.concatenate(
                [got[step, s, :, q * virt:(q + 1) * virt].astype(jnp.float32) for s in range(n)],
                axis=1,
            )
            value = (partial_sum - occupied[q * rows:(q + 1) * rows]).astype(jnp.bfloat16)
            dressed[step * group + q] = value
            weight = jnp.sum(jnp.where(at_row & (lane == q), weights, 0.0))
            total = total + weight * value.astype(jnp.float32)
        fock_ref[...] = total
        return carry

    lax.fori_loop(0, steps, consume, 0)

    half_rows = rows // 2
    own_half = pl.ds(pl.multiple_of(core * half_rows, 8), half_rows)
    mate_half = pl.ds(pl.multiple_of((1 - core) * half_rows, 8), half_rows)

    def swap(k, value, partner):
        fock_sent[k] = value
        copy = remote(
            fock_sent.at[k], fock_got.at[k], fock_send.at[k], fock_recv.at[k], {"pb": partner}
        )
        copy.start()
        copy.wait()
        return fock_got[k]

    both = swap(0, fock_ref[mate_half, :], mate) + fock_ref[own_half, :]
    every = (swap(1, both, across) + both) * (2.0 / (batch * n_pb))
    fock_ref[own_half, :] = every
    fock_ref[mate_half, :] = swap(2, every, mate)


def fused(n, n_pb, group, chol_vv, chol_ov, chol_oo, chol_vo, amplitudes):
    batch, virt, whole_virt = chol_vv.shape
    rows, occ = chol_ov.shape[1], chol_oo.shape[2]
    steps = batch // group
    wide, deep = group * virt, group * rows
    lines = -(-steps // 8) * 8
    bf16, f32 = jnp.bfloat16, jnp.float32
    dma = pltpu.SemaphoreType.DMA
    hops = 3
    whole = pl.BlockSpec(memory_space=pltpu.VMEM)
    hbm = pl.BlockSpec(memory_space=pl.ANY)
    return pl.pallas_call(
        functools.partial(kernel, n, n_pb, group),
        out_shape=(
            pltpu.VMEM((batch, rows, whole_virt), bf16),
            jax.ShapeDtypeStruct((rows, whole_virt), f32),
        ),
        in_specs=[hbm, hbm, hbm, hbm, whole],
        out_specs=(whole, whole),
        scratch_shapes=[
            pltpu.VMEM((2, group, virt, whole_virt), bf16),
            pltpu.VMEM((2, group, rows, whole_virt), bf16),
            pltpu.VMEM((2, group, rows, occ), bf16),
            pltpu.VMEM((2, group, virt, occ), bf16),
            pltpu.VMEM((whole_virt, occ), bf16),
            pltpu.VMEM((n * deep, whole_virt), bf16),
            pltpu.VMEM((occ, whole_virt), f32),
            pltpu.VMEM((rows, occ), f32),
            pltpu.VMEM((steps, occ, wide + deep), bf16),
            pltpu.VMEM((steps, n, rows, wide + deep), bf16),
            pltpu.VMEM((lines, 128), f32),
            pltpu.VMEM((n - 1, lines, 128), f32),
            pltpu.VMEM((hops, rows // 2, whole_virt), f32),
            pltpu.VMEM((hops, rows // 2, whole_virt), f32),
            dma((2, 4)), dma, dma((3, n - 1)), dma((3, n - 1)),
            dma((steps, n - 1)), dma((steps, n - 1)),
            dma((n - 1,)), dma((n - 1,)), dma((hops,)), dma((hops,)),
        ],
        compiler_params=pltpu.CompilerParams(
            collective_id=0, has_side_effects=True, vmem_limit_bytes=59800 * 1024
        ),
    )(chol_vv, chol_ov, chol_oo, jnp.swapaxes(chol_vo, 1, 2), amplitudes.T)


def group_size(batch, virt, rows):
    for group in range(1, batch + 1):
        if batch % group == 0 and group * virt % 128 == 0 and group * rows % 128 == 0:
            return group
    return None


def solution(mesh):
    n, n_pb = mesh.shape["pq"], mesh.shape["pb"]
    in_specs = (
        P("pb", "pq", None),
        P("pb", "pq", None),
        P("pb", "pq", None),
        P("pb", None, "pq"),
        P(None, "pq"),
    )
    out_specs = (P("pb", "pq", None), P("pq", None))

    def body(chol_vv, chol_ov, chol_oo, chol_vo, amplitudes):
        batch, virt, unused = chol_vv.shape
        rows, occ = chol_ov.shape[1], chol_oo.shape[2]
        group = group_size(batch, virt, rows)
        fits = group is not None and group <= 8 and virt % 32 == 0 and rows % 16 == 0
        fits = fits and occ % 256 == 0 and n_pb == 4 and n > 1 and batch // group <= rows
        if fits:
            return fused(n, n_pb, group, chol_vv, chol_ov, chol_oo, chol_vo, amplitudes)
        return per_device(chol_vv, chol_ov, chol_oo, chol_vo, amplitudes)

    return jax.shard_map(
        body, mesh=mesh, in_specs=in_specs, out_specs=out_specs, check_vma=False
    )
```

profile of v0, /device:TPU:13, one launch (start us, length us, event | category | flops | bytes accessed | tf_op | source)
XLA Modules:
  0.0 157.6 jit_solution(17871313953726130883)
XLA Ops:
  0.6 153.9 %shard_map.68 = (bf16[44,32,1792]{2,1,0:T(8,128)(2,1)S(1)}, f32[32,1792]{1,0:T(8,128)}) custom-call(bf16[44,224,1792]{2,1,0:T(8,128)(2,1)} %vv_hbm.1, bf16[44,32,1792]{2,1,0:T(8,128)(2,1)} %ov_hbm.1, bf16[44,32,256]{2,1,0:T(8,128)(2,1)} %oo_hbm.1, bf16[44,224,256]{2,1,0:T(8,128)(2,1)} %bitcast.2, bf16[224,256]{1,0:T(8,128)(2,1)} %bitcast.3), custom_call_target="tpu_custom_call" | custom-call | tf_op jit(solution)/shard_map/pallas_call | solution.py:286
  154.6 0.0 copy-start
  154.6 2.3 %copy.9 = bf16[44,32,1792]{2,1,0:T(8,128)(2,1)} copy(bf16[44,32,1792]{2,1,0:T(8,128)(2,1)S(1)} %get-tuple-element.2) | data formatting | bytes 10092544
  156.9 0.0 copy-done
  156.9 0.7 copy.10
Async XLA Ops:
  154.6 2.3 %copy-start = (f32[32,1792]{1,0:T(8,128)S(1)}, f32[32,1792]{1,0:T(8,128)}, u32[]{:S(2)}) copy-start(f32[32,1792]{1,0:T(8,128)} %get-tuple-element.7) | copy-start | bytes 688132
where the time goes:
time: 158 us
  Pallas kernels  154 us (97%)
  local copies, waits for them, and re-layouts  2.99 us (2%)
    pallas_call x1, Pallas kernels, fused(): pl.pallas_call(functools.partial(kernel, n, n_pb, group), out_shape=(pltp...  154 us

commit v1 on v0

v1 whole, which is shorter than its diff:
```python
import functools

import jax
import jax.numpy as jnp
from jax import lax
from jax.experimental import pallas as pl
from jax.experimental.pallas import tpu as pltpu
from jax.sharding import PartitionSpec as P

MESH = pl.DeviceIdType.MESH


def per_device(chol_vv, chol_ov, chol_oo, chol_vo, amplitudes):
    batch = chol_vv.shape[0]
    occ_rows = chol_ov.shape[1]
    whole_amps = lax.all_gather(amplitudes, "pq", axis=1, tiled=True)
    lprime = (
        chol_oo.astype(jnp.float32)
        + jnp.einsum("qjb,ib->qji", chol_ov, whole_amps, preferred_element_type=jnp.float32)
    ).astype(jnp.bfloat16)
    direct = jnp.einsum("qab,ib->qia", chol_vv, whole_amps, preferred_element_type=jnp.float32)
    partial_sum = chol_vo.astype(jnp.float32) + direct
    occupied = jnp.einsum(
        "qji,ja->qia",
        lax.all_gather(lprime, "pq", axis=1, tiled=True),
        amplitudes,
        preferred_element_type=jnp.float32,
    )
    local_dressed = (partial_sum - occupied).astype(jnp.bfloat16)
    dressed = lax.all_to_all(local_dressed, "pq", split_axis=1, concat_axis=2, tiled=True)
    row_start = lax.axis_index("pq") * occ_rows
    own_amps = lax.dynamic_slice_in_dim(whole_amps, row_start, occ_rows, 0)
    local_coulomb = 2.0 * jnp.einsum(
        "qia,ia->q", dressed, own_amps, preferred_element_type=jnp.float32
    )
    coulomb = lax.psum(local_coulomb, "pq")
    local_fock = jnp.sum(coulomb[:, None, None] * dressed.astype(jnp.float32), axis=0)
    fock_ov = lax.psum(local_fock, "pb") / (batch * lax.axis_size("pb"))
    return (dressed, fock_ov)


def kernel(
    n, n_pb, group,
    vv_hbm, ov_hbm, oo_hbm, vo_hbm, amps_hbm,
    dressed, fock_ref,
    vv_buf, ov_buf, oo_buf, vo_buf, amps_t, amps, tiled, gram, occ_buf,
    sent, got, coul_sent, coul_got, part_sent, part_got, sums_sent, sums_got,
    load_sem, own_sem, gather_send, gather_recv, send_sem, recv_sem,
    coul_sem, part_sem, sums_sem, fock_sem,
):
    me = lax.axis_index("pq")
    mine = lax.axis_index("pb")
    batch, virt, whole_virt = vv_hbm.shape
    rows, occ = ov_hbm.shape[1], oo_hbm.shape[2]
    steps = batch // group
    last = steps - 1
    wide, deep = group * virt, group * rows
    span = wide + deep
    sub = rows // n_pb
    half_n = n // 2
    peers = [lax.rem(me + d, n) for d in range(1, n)]
    core, place = lax.rem(mine, 2), mine // 2
    mate, across = mine + 1 - 2 * core, lax.rem(mine + 2, 4)
    partners = [mate, across, lax.rem(mate + 2, 4)]

    barrier = pltpu.get_barrier_semaphore()
    for peer in peers:
        pl.semaphore_signal(barrier, inc=1, device_id={"pq": peer}, device_id_type=MESH)
    for partner in partners:
        pl.semaphore_signal(barrier, inc=1, device_id={"pb": partner}, device_id_type=MESH)

    own_block = pl.ds(pl.multiple_of(me * virt, 16), virt)
    own = pltpu.make_async_copy(amps_hbm, amps_t.at[own_block], own_sem)
    own.start()

    def loads(step, slot):
        part = pl.ds(step * group, group)
        pairs = ((vv_hbm, vv_buf), (ov_hbm, ov_buf), (oo_hbm, oo_buf), (vo_hbm, vo_buf))
        return [
            pltpu.make_async_copy(src.at[part], dst.at[slot], load_sem.at[slot, k])
            for k, (src, dst) in enumerate(pairs)
        ]

    for copy in loads(0, 0):
        copy.start()

    def remote(src, dst, send, recv, where):
        return pltpu.make_async_remote_copy(
            src_ref=src, dst_ref=dst, send_sem=send, recv_sem=recv,
            device_id=where, device_id_type=MESH,
        )

    half_virt, half_occ = virt // 2, occ // 2
    own_columns = pl.ds(pl.multiple_of(core * half_occ, 128), half_occ)

    def quarter(owner):
        first = pl.multiple_of(owner * virt + place * half_virt, 16)
        return amps_t.at[pl.ds(first, half_virt), own_columns]

    side = me // half_n
    spot = lax.rem(me, half_n)
    near = [(1 - side) * half_n + lax.rem(side * (half_n // 2) + k, half_n) for k in range(half_n)]
    home = [side * half_n + lax.rem(spot + d, half_n) for d in range(1, half_n)]
    targets = near[:half_n // 2] + home + near[half_n // 2:]

    def gather(stage, owner, ref, where):
        return remote(ref, ref, gather_send, gather_recv.at[stage, owner], where)

    own.wait()
    pl.semaphore_wait(barrier, len(peers) + len(partners))
    for peer in targets:
        gather(0, me, quarter(me), {"pq": peer}).start()

    def half(owner):
        block = pl.ds(pl.multiple_of(owner * virt, 16), virt)
        return amps_t.at[block, own_columns]

    for owner in home + near:
        gather(0, owner, quarter(owner), {"pq": owner}).wait_recv()
        gather(1, owner, quarter(owner), {"pb": across}).start()

    def turn(owner):
        gather(1, owner, quarter(owner), {"pb": across}).wait_recv()
        gather(2, owner, half(owner), {"pb": mate}).start()

    def close(owner):
        gather(2, owner, half(owner), {"pb": mate}).wait_recv()

    def message(step, d):
        return remote(
            sent.at[step, pl.ds(pl.multiple_of(peers[d] * rows, 16), rows)],
            got.at[step, me],
            send_sem, recv_sem.at[step], {"pq": peers[d]},
        )

    def last_message(d, columns, k):
        return remote(
            sent.at[last, pl.ds(pl.multiple_of(peers[d] * rows, 16), rows), columns],
            got.at[last, me, :, columns],
            send_sem, recv_sem.at[last + k], {"pq": peers[d]},
        )

    def arrived(ref, sem, where):
        remote(ref, ref, send_sem, sem, where).wait_recv()

    direct_columns, lprime_columns = pl.ds(0, wide), pl.ds(wide, deep)
    early, middle = min(last, 3), min(last, 7)

    def form(slot):
        vv = vv_buf[slot].reshape(wide, whole_virt)
        direct = jnp.dot(vv, amps_t[...], preferred_element_type=jnp.float32)
        direct = direct + vo_buf[slot].reshape(wide, occ).astype(jnp.float32)
        ov = ov_buf[slot].reshape(deep, whole_virt)
        lprime = jnp.dot(ov, amps_t[...], preferred_element_type=jnp.float32)
        lprime = lprime + oo_buf[slot].reshape(deep, occ).astype(jnp.float32)
        return direct, lprime

    def put(step, direct, lprime):
        sent[step, :, 0:wide] = direct.T.astype(jnp.bfloat16)
        sent[step, :, wide:span] = lprime.T.astype(jnp.bfloat16)
        got[step, me] = sent[step, pl.ds(pl.multiple_of(me * rows, 16), rows), :]

    def send(step, carry):
        for d in range(n - 1):
            message(step, d).start()
        return carry

    half_whole = whole_virt // 2

    def half_form(which, direct, lprime):
        part = pl.ds(pl.multiple_of(which * half_whole, 128), half_whole)
        block = amps_t[part, :]
        vv = vv_buf[0, :, :, part].reshape(wide, half_whole)
        ov = ov_buf[0, :, :, part].reshape(deep, half_whole)
        direct = direct + jnp.dot(vv, block, preferred_element_type=jnp.float32)
        lprime = lprime + jnp.dot(ov, block, preferred_element_type=jnp.float32)
        return direct, lprime

    for owner in home:
        turn(owner)
    for copy in loads(0, 0):
        copy.wait()
    for owner in home:
        close(owner)
    direct = vo_buf[0].reshape(wide, occ).astype(jnp.float32)
    lprime = oo_buf[0].reshape(deep, occ).astype(jnp.float32)
    direct, lprime = half_form(side, direct, lprime)
    for owner in near:
        turn(owner)
    for owner in near:
        close(owner)
    direct, lprime = half_form(1 - side, direct, lprime)
    put(0, direct, lprime)
    send(0, 0)
    whole_gather = amps_t.at[pl.ds(0, (n - 1) * virt), :]
    remote(whole_gather, whole_gather, gather_send, gather_recv.at[0, me], {"pb": mate}).wait_send()

    for s in range(n):
        block = amps_t[s * virt:(s + 1) * virt, :]
        amps_t_f32 = block.astype(jnp.float32)
        tiled[:, s * virt:(s + 1) * virt] = amps_t_f32.T
    for s in range(n):
        part = tiled[s * rows:(s + 1) * rows, :].astype(jnp.bfloat16)
        for q in range(group):
            amps[s * deep + q * rows:s * deep + (q + 1) * rows, :] = part
    own_rows = amps[pl.ds(pl.multiple_of(me * deep, 128), rows), :]
    gram[...] = jnp.dot(own_rows, amps_t[...], preferred_element_type=jnp.float32)
    coul_sent[...] = jnp.zeros_like(coul_sent)

    def produce(step, carry):
        slot = lax.rem(step, 2)

        @pl.when(step + 1 < steps)
        def _():
            for copy in loads(step + 1, 1 - slot):
                copy.start()

        @pl.when(step > 0)
        def _():
            for copy in loads(step, slot):
                copy.wait()

        direct, lprime = form(slot)

        @pl.when(step > 0)
        def _():
            put(step, direct, lprime)

        own_amps = amps_t[own_block, :].astype(jnp.float32)
        lane = lax.broadcasted_iota(jnp.int32, coul_sent.shape, 1)
        held = coul_sent[...]
        for q in range(group):
            from_direct = direct[q * virt:(q + 1) * virt] * own_amps
            from_occ = lprime[q * rows:(q + 1) * rows] * gram[...]
            value = jnp.sum(from_direct) - jnp.sum(from_occ)
            held = jnp.where(lane == step * group + q, value, held)
        coul_sent[...] = held

        @pl.when((step > 0) & (step < early))
        def _():
            send(step, 0)

        return carry

    lax.fori_loop(0, steps, produce, 0)

    for d in range(n - 1):
        remote(coul_sent, coul_got.at[me], coul_sem.at[0], coul_sem.at[1], {"pq": peers[d]}).start()
    lax.fori_loop(early, middle, send, 0)
    all_coul = coul_got.at[pl.ds(0, n - 1)]
    remote(all_coul, all_coul, coul_sem.at[0], coul_sem.at[1], {"pq": peers[0]}).wait()

    coulomb = coul_sent[...]
    for d in range(n - 1):
        coulomb = coulomb + coul_got[peers[d]]
    lines = -(-steps // 8) * 8
    spread = jnp.broadcast_to(coulomb, (lines, 128))
    lane = lax.broadcasted_iota(jnp.int32, (lines, 128), 1)
    first = lax.broadcasted_iota(jnp.int32, (lines, 128), 0) * group
    spread = jnp.where((lane >= first) & (lane < first + group), spread, 0.0)
    column = lax.broadcasted_iota(jnp.int32, (128, span), 1)
    vector = jnp.zeros((128, span), jnp.int32)
    for q in range(1, group):
        vector = vector + jnp.where((column >= q * virt) & (column < wide), 1, 0)
        vector = vector + jnp.where(column >= wide + q * rows, 1, 0)
    place_of = lax.rem(lax.broadcasted_iota(jnp.int32, (128, span), 0), group)
    pick = jnp.where(place_of == vector, 1.0, 0.0)
    weights = jnp.dot(
        spread, pick, preferred_element_type=jnp.float32, precision=lax.Precision.HIGHEST
    )

    def weigh(d, carry):
        block = pl.ds(pl.multiple_of(d * rows, 16), rows)
        total = jnp.zeros((rows, span), jnp.float32)
        for s in range(steps):
            total = total + weights[s:s + 1, :] * sent[s, block, :].astype(jnp.float32)
        from_direct = total[:, 0:virt]
        from_occ = total[:, wide:wide + rows]
        for q in range(1, group):
            from_direct = from_direct + total[:, q * virt:(q + 1) * virt]
            from_occ = from_occ + total[:, wide + q * rows:wide + (q + 1) * rows]
        total = jnp.concatenate([from_direct, from_occ], axis=1)
        for m in range(n_pb):
            part_sent[m, d] = total[m * sub:(m + 1) * sub]
        return carry

    lax.fori_loop(0, n, weigh, 0)

    for partner in partners:
        remote(
            part_sent.at[partner], part_got.at[mine], part_sem.at[0], part_sem.at[1], {"pb": partner}
        ).start()

    def consume(step, carry):
        @pl.when(step == min(2, last - 1))
        def _():
            three = part_got.at[pl.ds(0, n_pb - 1)]
            remote(three, three, part_sem.at[0], part_sem.at[1], {"pb": mate}).wait()
            total = part_sent[mine]
            for partner in partners:
                total = total + part_got[partner]
            total = total.astype(jnp.bfloat16)
            for s in range(n):
                sums_sent[s] = jnp.concatenate([total[s, :, 0:128], total[s, :, 128:256]], axis=0)
            sums_got[me] = sums_sent[me]
            for d in range(n - 1):
                remote(
                    sums_sent.at[peers[d]], sums_got.at[me], sums_sem.at[0], sums_sem.at[1],
                    {"pq": peers[d]},
                ).start()
            lax.fori_loop(middle, last, send, 0)
            for d in range(n - 1):
                last_message(d, lprime_columns, 0).start()
            for d in range(n - 1):
                last_message(d, direct_columns, 1).start()

        @pl.when(step == last - 1)
        def _():
            several = sums_got.at[pl.ds(0, n - 1)]
            remote(several, several, sums_sem.at[0], sums_sem.at[1], {"pq": peers[0]}).wait()
            pieces = [sums_got[s] for s in range(n)]
            pieces = [
                jnp.concatenate([piece[0:sub], piece[sub:2 * sub]], axis=1).astype(jnp.float32)
                for piece in pieces
            ]
            partial_sum = jnp.concatenate([piece[:, 0:virt] for piece in pieces], axis=1)
            from_occ = jnp.concatenate([piece[:, virt:virt + rows] for piece in pieces], axis=1)
            from_occ = jnp.dot(
                from_occ.astype(jnp.bfloat16), tiled[...].astype(jnp.bfloat16),
                preferred_element_type=jnp.float32,
            )
            strip = pl.ds(pl.multiple_of(mine * sub, 8), sub)
            fock_ref[strip, :] = (partial_sum - from_occ) * (2.0 / (batch * n_pb))
            for partner in partners:
                remote(
                    fock_ref.at[strip], fock_ref.at[strip], fock_sem.at[0], fock_sem.at[1],
                    {"pb": partner},
                ).start()

        arrived(got.at[step, pl.ds(0, n - 1)], recv_sem.at[step], {"pq": peers[0]})
        subtract(step)
        finish(step)
        return carry

    def subtract(step):
        lane_q = lax.broadcasted_iota(jnp.int32, (rows, deep), 1) // rows
        columns = []
        for s in range(n):
            piece = got[step, s, :, wide:span]
            columns.append(jnp.concatenate(
                [jnp.where(lane_q == q, piece, jnp.zeros_like(piece)) for q in range(group)], axis=0
            ))
        occ_buf[...] = jnp.dot(
            jnp.concatenate(columns, axis=1), amps[...], preferred_element_type=jnp.float32
        )

    def finish(step):
        for q in range(group):
            partial_sum = jnp.concatenate(
                [got[step, s, :, q * virt:(q + 1) * virt].astype(jnp.float32) for s in range(n)],
                axis=1,
            )
            value = partial_sum - occ_buf[q * rows:(q + 1) * rows, :]
            dressed[step * group + q] = value.astype(jnp.bfloat16)

    lax.fori_loop(0, last, consume, 0)
    arrived(
        got.at[last, pl.ds(0, n - 1), :, lprime_columns], recv_sem.at[last], {"pq": peers[0]}
    )
    subtract(last)
    strips = fock_ref.at[pl.ds(0, (n_pb - 1) * sub)]
    remote(strips, strips, fock_sem.at[0], fock_sem.at[1], {"pb": mate}).wait()
    arrived(
        got.at[last, pl.ds(0, n - 1), :, direct_columns], recv_sem.at[last + 1], {"pq": peers[0]}
    )
    finish(last)
    everything = sent.at[:, pl.ds(0, (n - 1) * rows), :]
    remote(everything, everything, send_sem, recv_sem.at[0], {"pq": peers[0]}).wait_send()


def fused(n, n_pb, group, chol_vv, chol_ov, chol_oo, chol_vo, amplitudes):
    batch, virt, whole_virt = chol_vv.shape
    rows, occ = chol_ov.shape[1], chol_oo.shape[2]
    steps = batch // group
    wide, deep = group * virt, group * rows
    sub = rows // n_pb
    bf16, f32 = jnp.bfloat16, jnp.float32
    dma = pltpu.SemaphoreType.DMA
    whole = pl.BlockSpec(memory_space=pltpu.VMEM)
    hbm = pl.BlockSpec(memory_space=pl.ANY)
    return pl.pallas_call(
        functools.partial(kernel, n, n_pb, group),
        out_shape=(
            pltpu.VMEM((batch, rows, whole_virt), bf16),
            pltpu.VMEM((rows, whole_virt), f32),
        ),
        in_specs=[hbm, hbm, hbm, hbm, hbm],
        out_specs=(whole, whole),
        scratch_shapes=[
            pltpu.VMEM((2, group, virt, whole_virt), bf16),
            pltpu.VMEM((2, group, rows, whole_virt), bf16),
            pltpu.VMEM((2, group, rows, occ), bf16),
            pltpu.VMEM((2, group, virt, occ), bf16),
            pltpu.VMEM((whole_virt, occ), bf16),
            pltpu.VMEM((n * deep, whole_virt), bf16),
            pltpu.VMEM((occ, whole_virt), f32),
            pltpu.VMEM((rows, occ), f32),
            pltpu.VMEM((deep, whole_virt), f32),
            pltpu.VMEM((steps, occ, wide + deep), bf16),
            pltpu.VMEM((steps, n, rows, wide + deep), bf16),
            pltpu.VMEM((1, 128), f32),
            pltpu.VMEM((n, 1, 128), f32),
            pltpu.VMEM((n_pb, n, sub, virt + rows), f32),
            pltpu.VMEM((n_pb, n, sub, virt + rows), f32),
            pltpu.VMEM((n, 2 * sub, 128), bf16),
            pltpu.VMEM((n, 2 * sub, 128), bf16),
            dma((2, 4)), dma, dma, dma((3, n)), dma, dma((steps + 1,)),
            dma((2,)), dma((2,)), dma((2,)), dma((2,)),
        ],
        compiler_params=pltpu.CompilerParams(
            collective_id=0, has_side_effects=True, vmem_limit_bytes=59800 * 1024
        ),
    )(chol_vv, chol_ov, chol_oo, jnp.swapaxes(chol_vo, 1, 2), amplitudes.T)


def group_size(batch, virt, rows):
    for group in range(1, batch + 1):
        if batch % group == 0 and group * virt % 128 == 0 and group * rows % 128 == 0:
            return group
    return None


def solution(mesh):
    n, n_pb = mesh.shape["pq"], mesh.shape["pb"]
    in_specs = (
        P("pb", "pq", None),
        P("pb", "pq", None),
        P("pb", "pq", None),
        P("pb", None, "pq"),
        P(None, "pq"),
    )
    out_specs = (P("pb", "pq", None), P("pq", None))

    def body(chol_vv, chol_ov, chol_oo, chol_vo, amplitudes):
        batch, virt, whole_virt = chol_vv.shape
        rows, occ = chol_ov.shape[1], chol_oo.shape[2]
        group = group_size(batch, virt, rows)
        fits = group is not None and group <= 8 and virt % 32 == 0 and rows % 16 == 0
        fits = fits and occ % 256 == 0 and n_pb == 4 and n > 1 and n % 4 == 0
        fits = fits and virt + rows == 256 and rows == 8 * n_pb and 3 <= batch // group <= 16
        fits = fits and batch <= 128 and whole_virt % 256 == 0
        if fits:
            return fused(n, n_pb, group, chol_vv, chol_ov, chol_oo, chol_vo, amplitudes)
        return per_device(chol_vv, chol_ov, chol_oo, chol_vo, amplitudes)

    return jax.shard_map(
        body, mesh=mesh, in_specs=in_specs, out_specs=out_specs, check_vma=False
    )
```

time: 158 us -> 147 us (0.930)
  Pallas kernels: 154 us -> 141 us
    pallas_call x1, Pallas kernels: 154 us -> 141 us  [fused(): pl.pallas_call(functools.partial(kernel, n, n_pb, group), out_shape=(pltp...]
where the time goes in v1:
time: 147 us; the launch traced here: 145 us
  Pallas kernels  141 us (96%)
  local copies, waits for them, and re-layouts  2.98 us (2%)
    pallas_call x1, Pallas kernels, fused(): pl.pallas_call(functools.partial(kernel, n, n_pb, group), out_shape=(pltp...  141 us
    unnamed x2, local copies, waits for them, and re-layouts  2.98 us

profile of v1, /device:TPU:13, one launch (start us, length us, event | category | flops | bytes accessed | tf_op | source)
XLA Modules:
  0.0 145.1 jit_solution(11429093246824242546)
XLA Ops:
  0.6 141.5 %shard_map.68 = (bf16[44,32,1792]{2,1,0:T(8,128)(2,1)S(1)}, f32[32,1792]{1,0:T(8,128)S(1)}) custom-call(bf16[44,224,1792]{2,1,0:T(8,128)(2,1)} %vv_hbm.1, bf16[44,32,1792]{2,1,0:T(8,128)(2,1)} %ov_hbm.1, bf16[44,32,256]{2,1,0:T(8,128)(2,1)} %oo_hbm.1, bf16[44,224,256]{2,1,0:T(8,128)(2,1)} %bitcast.2, bf16[224,256]{1,0:T(8,128)(2,1)} %bitcast.3), custom_call_target="tpu_custom_call" | custom-call | tf_op jit(solution)/shard_map/pallas_call | solution.py:391
  142.1 2.3 %copy.9 = bf16[44,32,1792]{2,1,0:T(8,128)(2,1)} copy(bf16[44,32,1792]{2,1,0:T(8,128)(2,1)S(1)} %get-tuple-element.2) | data formatting | bytes 10092544
  144.4 0.7 copy.10

commit v2 on v1

--- a/solution.py
+++ b/solution.py
@@ -46,7 +46,7 @@
     vv_buf, ov_buf, oo_buf, vo_buf, amps_t, amps, tiled, gram, occ_buf,
     sent, got, coul_sent, coul_got, part_sent, part_got, sums_sent, sums_got,
     load_sem, own_sem, gather_send, gather_recv, send_sem, recv_sem,
-    coul_sem, part_sem, sums_sem, fock_sem,
+    coul_sem, part_sem, sums_sem, fock_sem, ready,
 ):
     me = lax.axis_index("pq")
     mine = lax.axis_index("pb")
@@ -57,17 +57,21 @@
     wide, deep = group * virt, group * rows
     span = wide + deep
     sub = rows // n_pb
-    half_n = n // 2
+    half_n, quarter_n = n // 2, n // 4
     peers = [lax.rem(me + d, n) for d in range(1, n)]
-    core, place = lax.rem(mine, 2), mine // 2
+    core = lax.rem(mine, 2)
     mate, across = mine + 1 - 2 * core, lax.rem(mine + 2, 4)
     partners = [mate, across, lax.rem(mate + 2, 4)]
 
     barrier = pltpu.get_barrier_semaphore()
     for peer in peers:
-        pl.semaphore_signal(barrier, inc=1, device_id={"pq": peer}, device_id_type=MESH)
+        @pl.when(peer > me)
+        def _():
+            pl.semaphore_signal(barrier, inc=1, device_id={"pq": peer}, device_id_type=MESH)
     for partner in partners:
-        pl.semaphore_signal(barrier, inc=1, device_id={"pb": partner}, device_id_type=MESH)
+        @pl.when(partner > mine)
+        def _():
+            pl.semaphore_signal(barrier, inc=1, device_id={"pb": partner}, device_id_type=MESH)
 
     own_block = pl.ds(pl.multiple_of(me * virt, 16), virt)
     own = pltpu.make_async_copy(amps_hbm, amps_t.at[own_block], own_sem)
@@ -91,46 +95,83 @@
         )
 
     half_virt, half_occ = virt // 2, occ // 2
-    own_columns = pl.ds(pl.multiple_of(core * half_occ, 128), half_occ)
-
-    def quarter(owner):
-        first = pl.multiple_of(owner * virt + place * half_virt, 16)
-        return amps_t.at[pl.ds(first, half_virt), own_columns]
-
-    side = me // half_n
-    spot = lax.rem(me, half_n)
-    near = [(1 - side) * half_n + lax.rem(side * (half_n // 2) + k, half_n) for k in range(half_n)]
+    side, spot = me // half_n, lax.rem(me, half_n)
+    other = 1 - side
     home = [side * half_n + lax.rem(spot + d, half_n) for d in range(1, half_n)]
-    targets = near[:half_n // 2] + home + near[half_n // 2:]
-
-    def gather(stage, owner, ref, where):
-        return remote(ref, ref, gather_send, gather_recv.at[stage, owner], where)
-
+    cross = [other * half_n + lax.rem(side * quarter_n + k, half_n) for k in range(half_n)]
+    near = [cross[0] + lax.rem(spot + k, quarter_n) for k in range(quarter_n)]
+    targets = [
+        side * second + other * first for first, second in zip(home + near, near + home)
+    ]
+    is_near = spot // quarter_n == other
+    beyond = lax.rem(me + n + quarter_n * (2 * side - 1), n)
+
+    @pl.when(me + mine > 0)
+    def _():
+        pl.semaphore_wait(barrier, me + mine)
+
+    for peer in peers:
+        @pl.when(peer < me)
+        def _():
+            pl.semaphore_signal(ready.at[me], inc=1, device_id={"pq": peer}, device_id_type=MESH)
+    for partner in partners:
+        @pl.when(partner < mine)
+        def _():
+            pl.semaphore_signal(
+                ready.at[n + mine], inc=1, device_id={"pb": partner}, device_id_type=MESH
+            )
+
+    def greet(peer):
+        @pl.when(peer > me)
+        def _():
+            pl.semaphore_wait(ready.at[peer], 1)
+
+    def greet_partner(partner):
+        @pl.when(partner > mine)
+        def _():
+            pl.semaphore_wait(ready.at[n + partner], 1)
+
+    def columns_of(which):
+        return pl.ds(pl.multiple_of(which * half_occ, 128), half_occ)
+
+    def piece(owner, which):
+        first = pl.multiple_of(owner * virt + core * half_virt, 16)
+        return amps_t.at[pl.ds(first, half_virt), columns_of(which)]
+
+    def hop(owner, turn, which, peer):
+        ref = piece(owner, which)
+        return remote(ref, ref, gather_send, gather_recv.at[turn, owner], {"pq": peer})
+
+    def swap(owner, turn):
+        ref = piece(owner, turns[turn])
+        return remote(ref, ref, gather_send, gather_recv.at[2 + turn, owner], {"pb": mate})
+
+    turns = [other, side]
     own.wait()
-    pl.semaphore_wait(barrier, len(peers) + len(partners))
     for peer in targets:
-        gather(0, me, quarter(me), {"pq": peer}).start()
-
-    def half(owner):
-        block = pl.ds(pl.multiple_of(owner * virt, 16), virt)
-        return amps_t.at[block, own_columns]
-
-    for owner in home + near:
-        gather(0, owner, quarter(owner), {"pq": owner}).wait_recv()
-        gather(1, owner, quarter(owner), {"pb": across}).start()
-
-    def turn(owner):
-        gather(1, owner, quarter(owner), {"pb": across}).wait_recv()
-        gather(2, owner, half(owner), {"pb": mate}).start()
-
-    def close(owner):
-        gather(2, owner, half(owner), {"pb": mate}).wait_recv()
-
-    def message(step, d):
+        greet(peer)
+        hop(me, 0, 1 - peer // half_n, peer).start()
+    for peer in targets:
+        hop(me, 1, peer // half_n, peer).start()
+
+    def pass_on(owners, turn, relay):
+        for owner in owners:
+            hop(owner, turn, turns[turn], owner).wait_recv()
+            if relay:
+                @pl.when(is_near)
+                def _():
+                    hop(owner, turn, turns[turn], beyond).start()
+            swap(owner, turn).start()
+
+    def close(owners, turn):
+        for owner in owners:
+            swap(owner, turn).wait_recv()
+
+    def message(step, peer):
         return remote(
-            sent.at[step, pl.ds(pl.multiple_of(peers[d] * rows, 16), rows)],
+            sent.at[step, pl.ds(pl.multiple_of(peer * rows, 16), rows)],
             got.at[step, me],
-            send_sem, recv_sem.at[step], {"pq": peers[d]},
+            send_sem, recv_sem.at[step], {"pq": peer},
         )
 
     def last_message(d, columns, k):
@@ -161,39 +202,66 @@
         got[step, me] = sent[step, pl.ds(pl.multiple_of(me * rows, 16), rows), :]
 
     def send(step, carry):
-        for d in range(n - 1):
-            message(step, d).start()
+        for peer in peers:
+            message(step, peer).start()
         return carry
 
     half_whole = whole_virt // 2
 
-    def half_form(which, direct, lprime):
-        part = pl.ds(pl.multiple_of(which * half_whole, 128), half_whole)
-        block = amps_t[part, :]
+    def half_form(part, which, direct, lprime):
+        part = pl.ds(pl.multiple_of(part * half_whole, 128), half_whole)
+        block = amps_t[part, columns_of(which)]
         vv = vv_buf[0, :, :, part].reshape(wide, half_whole)
         ov = ov_buf[0, :, :, part].reshape(deep, half_whole)
         direct = direct + jnp.dot(vv, block, preferred_element_type=jnp.float32)
         lprime = lprime + jnp.dot(ov, block, preferred_element_type=jnp.float32)
         return direct, lprime
 
-    for owner in home:
-        turn(owner)
+    def start_form(which):
+        direct = vo_buf[0, :, :, columns_of(which)].reshape(wide, half_occ).astype(jnp.float32)
+        lprime = oo_buf[0, :, :, columns_of(which)].reshape(deep, half_occ).astype(jnp.float32)
+        return half_form(side, which, direct, lprime)
+
+    def put_half(which, direct, lprime):
+        sent[0, columns_of(which), 0:wide] = direct.T.astype(jnp.bfloat16)
+        sent[0, columns_of(which), wide:span] = lprime.T.astype(jnp.bfloat16)
+
+    greet_partner(mate)
+    pass_on(home, 0, False)
     for copy in loads(0, 0):
         copy.wait()
-    for owner in home:
-        close(owner)
-    direct = vo_buf[0].reshape(wide, occ).astype(jnp.float32)
-    lprime = oo_buf[0].reshape(deep, occ).astype(jnp.float32)
-    direct, lprime = half_form(side, direct, lprime)
-    for owner in near:
-        turn(owner)
-    for owner in near:
-        close(owner)
-    direct, lprime = half_form(1 - side, direct, lprime)
-    put(0, direct, lprime)
-    send(0, 0)
-    whole_gather = amps_t.at[pl.ds(0, (n - 1) * virt), :]
-    remote(whole_gather, whole_gather, gather_send, gather_recv.at[0, me], {"pb": mate}).wait_send()
+    close(home, 0)
+    direct, lprime = start_form(other)
+
+    pass_on(cross, 0, True)
+    close(cross, 0)
+    direct, lprime = half_form(other, other, direct, lprime)
+    put_half(other, direct, lprime)
+    for peer in cross[quarter_n:]:
+        greet(peer)
+    for peer in cross:
+        message(0, peer).start()
+    pass_on(home, 1, False)
+    pass_on(cross, 1, True)
+    close(home + cross, 1)
+    direct, lprime = start_form(side)
+    direct, lprime = half_form(other, side, direct, lprime)
+    put_half(side, direct, lprime)
+    got[0, me] = sent[0, pl.ds(pl.multiple_of(me * rows, 16), rows), :]
+    for peer in home:
+        message(0, peer).start()
+    for partner in partners[1:]:
+        greet_partner(partner)
+
+    @pl.when(is_near)
+    def _():
+        ref = amps_t
+        remote(ref, ref, gather_send, gather_recv.at[0, me], {"pb": mate}).wait_send()
+
+    @pl.when(jnp.logical_not(is_near))
+    def _():
+        ref = amps_t.at[pl.ds(0, (n - 2) * virt), :]
+        remote(ref, ref, gather_send, gather_recv.at[0, me], {"pb": mate}).wait_send()
 
     for s in range(n):
         block = amps_t[s * virt:(s + 1) * virt, :]
@@ -414,8 +482,9 @@
             pltpu.VMEM((n_pb, n, sub, virt + rows), f32),
             pltpu.VMEM((n, 2 * sub, 128), bf16),
             pltpu.VMEM((n, 2 * sub, 128), bf16),
-            dma((2, 4)), dma, dma, dma((3, n)), dma, dma((steps + 1,)),
+            dma((2, 4)), dma, dma, dma((4, n)), dma, dma((steps + 1,)),
             dma((2,)), dma((2,)), dma((2,)), dma((2,)),
+            pltpu.SemaphoreType.REGULAR((n + n_pb,)),
         ],
         compiler_params=pltpu.CompilerParams(
             collective_id=0, has_side_effects=True, vmem_limit_bytes=59800 * 1024
@@ -446,7 +515,7 @@
         rows, occ = chol_ov.shape[1], chol_oo.shape[2]
         group = group_size(batch, virt, rows)
         fits = group is not None and group <= 8 and virt % 32 == 0 and rows % 16 == 0
-        fits = fits and occ % 256 == 0 and n_pb == 4 and n > 1 and n % 4 == 0
+        fits = fits and occ % 256 == 0 and n_pb == 4 and n == 8
         fits = fits and virt + rows == 256 and rows == 8 * n_pb and 3 <= batch // group <= 16
         fits = fits and batch <= 128 and whole_virt % 256 == 0
         if fits:

time: 147 us -> 144 us (0.980)
  Pallas kernels: 141 us -> 139 us
    pallas_call x1, Pallas kernels: 141 us -> 139 us  [fused(): pl.pallas_call(functools.partial(kernel, n, n_pb, group), out_shape=(pltp...]
where the time goes in v2:
time: 144 us; the launch traced here: 142 us
  Pallas kernels  139 us (97%)
  local copies, waits for them, and re-layouts  2.98 us (2%)
    pallas_call x1, Pallas kernels, fused(): pl.pallas_call(functools.partial(kernel, n, n_pb, group), out_shape=(pltp...  139 us
    unnamed x2, local copies, waits for them, and re-layouts  2.98 us

profile of v2, /device:TPU:13, one launch (start us, length us, event | category | flops | bytes accessed | tf_op | source)
XLA Modules:
  0.0 142.2 jit_solution(8169015327129716475)
XLA Ops:
  0.6 138.5 %shard_map.68 = (bf16[44,32,1792]{2,1,0:T(8,128)(2,1)S(1)}, f32[32,1792]{1,0:T(8,128)S(1)}) custom-call(bf16[44,224,1792]{2,1,0:T(8,128)(2,1)} %vv_hbm.1, bf16[44,32,1792]{2,1,0:T(8,128)(2,1)} %ov_hbm.1, bf16[44,32,256]{2,1,0:T(8,128)(2,1)} %oo_hbm.1, bf16[44,224,256]{2,1,0:T(8,128)(2,1)} %bitcast.2, bf16[224,256]{1,0:T(8,128)(2,1)} %bitcast.3), custom_call_target="tpu_custom_call" | custom-call | tf_op jit(solution)/shard_map/pallas_call | solution.py:459
  139.2 2.3 %copy.9 = bf16[44,32,1792]{2,1,0:T(8,128)(2,1)} copy(bf16[44,32,1792]{2,1,0:T(8,128)(2,1)S(1)} %get-tuple-element.2) | data formatting | bytes 10092544
  141.5 0.7 copy.10

commit v3 on v2

--- a/solution.py
+++ b/solution.py
@@ -42,9 +42,9 @@
 def kernel(
     n, n_pb, group,
     vv_hbm, ov_hbm, oo_hbm, vo_hbm, amps_hbm,
-    dressed, fock_ref,
-    vv_buf, ov_buf, oo_buf, vo_buf, amps_t, amps, tiled, gram, occ_buf,
-    sent, got, coul_sent, coul_got, part_sent, part_got, sums_sent, sums_got,
+    dressed, fock_ref, got, occ_buf,
+    vv_buf, ov_buf, oo_buf, vo_buf, amps_t, amps, tiled, gram,
+    sent, coul_sent, coul_got, part_sent, part_got, sums_sent, sums_got,
     load_sem, own_sem, gather_send, gather_recv, send_sem, recv_sem,
     coul_sem, part_sem, sums_sem, fock_sem, ready,
 ):
@@ -85,9 +85,6 @@
             for k, (src, dst) in enumerate(pairs)
         ]
 
-    for copy in loads(0, 0):
-        copy.start()
-
     def remote(src, dst, send, recv, where):
         return pltpu.make_async_remote_copy(
             src_ref=src, dst_ref=dst, send_sem=send, recv_sem=recv,
@@ -101,7 +98,7 @@
     cross = [other * half_n + lax.rem(side * quarter_n + k, half_n) for k in range(half_n)]
     near = [cross[0] + lax.rem(spot + k, quarter_n) for k in range(quarter_n)]
     targets = [
-        side * second + other * first for first, second in zip(home + near, near + home)
+        second for first, second in zip(home + near, near + home)
     ]
     is_near = spot // quarter_n == other
     beyond = lax.rem(me + n + quarter_n * (2 * side - 1), n)
@@ -151,8 +148,8 @@
     for peer in targets:
         greet(peer)
         hop(me, 0, 1 - peer // half_n, peer).start()
-    for peer in targets:
-        hop(me, 1, peer // half_n, peer).start()
+    for copy in loads(0, 0):
+        copy.start()
 
     def pass_on(owners, turn, relay):
         for owner in owners:
@@ -167,25 +164,28 @@
         for owner in owners:
             swap(owner, turn).wait_recv()
 
-    def message(step, peer):
+    early, middle = min(last, 3), min(last, 7)
+    chunks = [(step, 1) for step in range(early)]
+    chunks += [(step, 1) for step in range(early, last)]
+    chunks = [(first, count) for first, count in chunks if count > 0]
+
+    def message(k, peer):
+        first, count = chunks[k]
         return remote(
-            sent.at[step, pl.ds(pl.multiple_of(peer * rows, 16), rows)],
-            got.at[step, me],
-            send_sem, recv_sem.at[step], {"pq": peer},
+            sent.at[peer, pl.ds(first, count)], got.at[me, pl.ds(first, count)],
+            send_sem, recv_sem.at[k], {"pq": peer},
         )
 
-    def last_message(d, columns, k):
+    def last_message(peer, columns, k):
         return remote(
-            sent.at[last, pl.ds(pl.multiple_of(peers[d] * rows, 16), rows), columns],
-            got.at[last, me, :, columns],
-            send_sem, recv_sem.at[last + k], {"pq": peers[d]},
+            sent.at[peer, last, :, columns], got.at[me, last, :, columns],
+            send_sem, recv_sem.at[len(chunks) + k], {"pq": peer},
         )
 
     def arrived(ref, sem, where):
         remote(ref, ref, send_sem, sem, where).wait_recv()
 
     direct_columns, lprime_columns = pl.ds(0, wide), pl.ds(wide, deep)
-    early, middle = min(last, 3), min(last, 7)
 
     def form(slot):
         vv = vv_buf[slot].reshape(wide, whole_virt)
@@ -197,14 +197,15 @@
         return direct, lprime
 
     def put(step, direct, lprime):
-        sent[step, :, 0:wide] = direct.T.astype(jnp.bfloat16)
-        sent[step, :, wide:span] = lprime.T.astype(jnp.bfloat16)
-        got[step, me] = sent[step, pl.ds(pl.multiple_of(me * rows, 16), rows), :]
-
-    def send(step, carry):
+        turned = direct.T.astype(jnp.bfloat16)
+        sent[:, step, :, 0:wide] = turned.reshape(n, rows, wide)
+        turned = lprime.T.astype(jnp.bfloat16)
+        sent[:, step, :, wide:span] = turned.reshape(n, rows, deep)
+        got[me, step] = sent[me, step]
+
+    def send(k):
         for peer in peers:
-            message(step, peer).start()
-        return carry
+            message(k, peer).start()
 
     half_whole = whole_virt // 2
 
@@ -223,17 +224,21 @@
         return half_form(side, which, direct, lprime)
 
     def put_half(which, direct, lprime):
-        sent[0, columns_of(which), 0:wide] = direct.T.astype(jnp.bfloat16)
-        sent[0, columns_of(which), wide:span] = lprime.T.astype(jnp.bfloat16)
+        part = pl.ds(which * half_n, half_n)
+        turned = direct.T.astype(jnp.bfloat16)
+        sent[part, 0, :, 0:wide] = turned.reshape(half_n, rows, wide)
+        turned = lprime.T.astype(jnp.bfloat16)
+        sent[part, 0, :, wide:span] = turned.reshape(half_n, rows, deep)
 
     greet_partner(mate)
     pass_on(home, 0, False)
+    for peer in targets:
+        hop(me, 1, peer // half_n, peer).start()
+    pass_on(cross, 0, True)
     for copy in loads(0, 0):
         copy.wait()
     close(home, 0)
     direct, lprime = start_form(other)
-
-    pass_on(cross, 0, True)
     close(cross, 0)
     direct, lprime = half_form(other, other, direct, lprime)
     put_half(other, direct, lprime)
@@ -247,7 +252,7 @@
     direct, lprime = start_form(side)
     direct, lprime = half_form(other, side, direct, lprime)
     put_half(side, direct, lprime)
-    got[0, me] = sent[0, pl.ds(pl.multiple_of(me * rows, 16), rows), :]
+    got[me, 0] = sent[me, 0]
     for peer in home:
         message(0, peer).start()
     for partner in partners[1:]:
@@ -304,9 +309,10 @@
             held = jnp.where(lane == step * group + q, value, held)
         coul_sent[...] = held
 
-        @pl.when((step > 0) & (step < early))
-        def _():
-            send(step, 0)
+        for k in range(1, early):
+            @pl.when(step == k)
+            def _():
+                send(k)
 
         return carry
 
@@ -314,7 +320,9 @@
 
     for d in range(n - 1):
         remote(coul_sent, coul_got.at[me], coul_sem.at[0], coul_sem.at[1], {"pq": peers[d]}).start()
-    lax.fori_loop(early, middle, send, 0)
+    for k, (first, count) in enumerate(chunks):
+        if early <= first < middle:
+            send(k)
     all_coul = coul_got.at[pl.ds(0, n - 1)]
     remote(all_coul, all_coul, coul_sem.at[0], coul_sem.at[1], {"pq": peers[0]}).wait()
 
@@ -338,10 +346,9 @@
     )
 
     def weigh(d, carry):
-        block = pl.ds(pl.multiple_of(d * rows, 16), rows)
         total = jnp.zeros((rows, span), jnp.float32)
         for s in range(steps):
-            total = total + weights[s:s + 1, :] * sent[s, block, :].astype(jnp.float32)
+            total = total + weights[s:s + 1, :] * sent[d, s].astype(jnp.float32)
         from_direct = total[:, 0:virt]
         from_occ = total[:, wide:wide + rows]
         for q in range(1, group):
@@ -376,11 +383,13 @@
                     sums_sent.at[peers[d]], sums_got.at[me], sums_sem.at[0], sums_sem.at[1],
                     {"pq": peers[d]},
                 ).start()
-            lax.fori_loop(middle, last, send, 0)
-            for d in range(n - 1):
-                last_message(d, lprime_columns, 0).start()
-            for d in range(n - 1):
-                last_message(d, direct_columns, 1).start()
+            for k, (first, count) in enumerate(chunks):
+                if first >= middle:
+                    send(k)
+            for peer in peers:
+                last_message(peer, lprime_columns, 0).start()
+            for peer in peers:
+                last_message(peer, direct_columns, 1).start()
 
         @pl.when(step == last - 1)
         def _():
@@ -405,7 +414,12 @@
                     {"pb": partner},
                 ).start()
 
-        arrived(got.at[step, pl.ds(0, n - 1)], recv_sem.at[step], {"pq": peers[0]})
+        for k, (first, count) in enumerate(chunks):
+            @pl.when(step == first)
+            def _():
+                ref = got.at[pl.ds(0, n - 1), pl.ds(first, count)]
+                arrived(ref, recv_sem.at[k], {"pq": peers[0]})
+
         subtract(step)
         finish(step)
         return carry
@@ -414,7 +428,7 @@
         lane_q = lax.broadcasted_iota(jnp.int32, (rows, deep), 1) // rows
         columns = []
         for s in range(n):
-            piece = got[step, s, :, wide:span]
+            piece = got[s, step, :, wide:span]
             columns.append(jnp.concatenate(
                 [jnp.where(lane_q == q, piece, jnp.zeros_like(piece)) for q in range(group)], axis=0
             ))
@@ -424,26 +438,49 @@
 
     def finish(step):
         for q in range(group):
-            partial_sum = jnp.concatenate(
-                [got[step, s, :, q * virt:(q + 1) * virt].astype(jnp.float32) for s in range(n)],
-                axis=1,
-            )
-            value = partial_sum - occ_buf[q * rows:(q + 1) * rows, :]
-            dressed[step * group + q] = value.astype(jnp.bfloat16)
+            dressed[step * group + q] = finished(n, virt, rows, got, occ_buf, step, q)
 
     lax.fori_loop(0, last, consume, 0)
-    arrived(
-        got.at[last, pl.ds(0, n - 1), :, lprime_columns], recv_sem.at[last], {"pq": peers[0]}
-    )
+    ref = got.at[pl.ds(0, n - 1), last, :, lprime_columns]
+    arrived(ref, recv_sem.at[len(chunks)], {"pq": peers[0]})
     subtract(last)
     strips = fock_ref.at[pl.ds(0, (n_pb - 1) * sub)]
     remote(strips, strips, fock_sem.at[0], fock_sem.at[1], {"pb": mate}).wait()
-    arrived(
-        got.at[last, pl.ds(0, n - 1), :, direct_columns], recv_sem.at[last + 1], {"pq": peers[0]}
-    )
-    finish(last)
-    everything = sent.at[:, pl.ds(0, (n - 1) * rows), :]
+    everything = sent.at[pl.ds(0, n - 1)]
     remote(everything, everything, send_sem, recv_sem.at[0], {"pq": peers[0]}).wait_send()
+    ref = got.at[pl.ds(0, n - 1), last, :, direct_columns]
+    arrived(ref, recv_sem.at[len(chunks) + 1], {"pq": peers[0]})
+
+
+def finished(n, virt, rows, got, occ_buf, step, q):
+    partial_sum = jnp.concatenate(
+        [got[s, step, :, q * virt:(q + 1) * virt].astype(jnp.float32) for s in range(n)], axis=1
+    )
+    return (partial_sum - occ_buf[q * rows:(q + 1) * rows, :]).astype(jnp.bfloat16)
+
+
+def store(n, virt, group, dressed, fock, got, occ_buf, dressed_out, fock_out, tail, sems):
+    batch, rows = dressed.shape[:2]
+    done = batch - group
+    parts = 2
+    size = done // parts
+    copies = [
+        pltpu.make_async_copy(
+            dressed.at[pl.ds(p * size, size)], dressed_out.at[pl.ds(p * size, size)], sems.at[p]
+        )
+        for p in range(parts)
+    ]
+    copies.append(pltpu.make_async_copy(fock, fock_out, sems.at[parts]))
+    for copy in copies:
+        copy.start()
+    for q in range(group):
+        tail[q] = finished(n, virt, rows, got, occ_buf, batch // group - 1, q)
+    copies.append(
+        pltpu.make_async_copy(tail, dressed_out.at[pl.ds(done, group)], sems.at[parts + 1])
+    )
+    copies[-1].start()
+    for copy in copies:
+        copy.wait()
 
 
 def fused(n, n_pb, group, chol_vv, chol_ov, chol_oo, chol_vo, amplitudes):
@@ -456,14 +493,16 @@
     dma = pltpu.SemaphoreType.DMA
     whole = pl.BlockSpec(memory_space=pltpu.VMEM)
     hbm = pl.BlockSpec(memory_space=pl.ANY)
-    return pl.pallas_call(
+    dressed, fock, got, occupied = pl.pallas_call(
         functools.partial(kernel, n, n_pb, group),
         out_shape=(
             pltpu.VMEM((batch, rows, whole_virt), bf16),
             pltpu.VMEM((rows, whole_virt), f32),
+            pltpu.VMEM((n, steps, rows, wide + deep), bf16),
+            pltpu.VMEM((deep, whole_virt), f32),
         ),
         in_specs=[hbm, hbm, hbm, hbm, hbm],
-        out_specs=(whole, whole),
+        out_specs=(whole, whole, whole, whole),
         scratch_shapes=[
             pltpu.VMEM((2, group, virt, whole_virt), bf16),
             pltpu.VMEM((2, group, rows, whole_virt), bf16),
@@ -473,23 +512,32 @@
             pltpu.VMEM((n * deep, whole_virt), bf16),
             pltpu.VMEM((occ, whole_virt), f32),
             pltpu.VMEM((rows, occ), f32),
-            pltpu.VMEM((deep, whole_virt), f32),
-            pltpu.VMEM((steps, occ, wide + deep), bf16),
-            pltpu.VMEM((steps, n, rows, wide + deep), bf16),
+            pltpu.VMEM((n, steps, rows, wide + deep), bf16),
             pltpu.VMEM((1, 128), f32),
             pltpu.VMEM((n, 1, 128), f32),
             pltpu.VMEM((n_pb, n, sub, virt + rows), f32),
             pltpu.VMEM((n_pb, n, sub, virt + rows), f32),
             pltpu.VMEM((n, 2 * sub, 128), bf16),
             pltpu.VMEM((n, 2 * sub, 128), bf16),
-            dma((2, 4)), dma, dma, dma((4, n)), dma, dma((steps + 1,)),
+            dma((2, 4)), dma, dma, dma((4, n)), dma, dma((13,)),
             dma((2,)), dma((2,)), dma((2,)), dma((2,)),
             pltpu.SemaphoreType.REGULAR((n + n_pb,)),
         ],
         compiler_params=pltpu.CompilerParams(
-            collective_id=0, has_side_effects=True, vmem_limit_bytes=59800 * 1024
+            collective_id=0, has_side_effects=True, vmem_limit_bytes=48 * 1024 * 1024
         ),
     )(chol_vv, chol_ov, chol_oo, jnp.swapaxes(chol_vo, 1, 2), amplitudes.T)
+    return pl.pallas_call(
+        functools.partial(store, n, virt, group),
+        out_shape=(
+            jax.ShapeDtypeStruct(dressed.shape, bf16),
+            jax.ShapeDtypeStruct(fock.shape, f32),
+        ),
+        in_specs=[whole, whole, whole, whole],
+        out_specs=(hbm, hbm),
+        scratch_shapes=[pltpu.VMEM((group, rows, whole_virt), bf16), dma((4,))],
+        compiler_params=pltpu.CompilerParams(vmem_limit_bytes=8 * 1024 * 1024),
+    )(dressed, fock, got, occupied)
 
 
 def group_size(batch, virt, rows):

time: 144 us -> 141 us (0.979)
  local copies, waits for them, and re-layouts: 2.98 us -> 0 us
    unnamed x2 -> x0, local copies, waits for them, and re-layouts: 2.98 us -> none
    pallas_call x0 -> x1, Pallas kernels: none -> 2.38 us  [fused(): pl.pallas_call(functools.partial(store, n, virt, group), out_shape=(jax.S...]
where the time goes in v3:
time: 141 us
  Pallas kernels  140 us (99%)
    pallas_call x1, Pallas kernels, fused(): pl.pallas_call(functools.partial(kernel, n, n_pb, group), out_shape=(pltp...  138 us

profile of v3, /device:TPU:13, one launch (start us, length us, event | category | flops | bytes accessed | tf_op | source)
XLA Modules:
  0.0 140.6 jit_solution(14583212704159519186)
XLA Ops:
  0.6 137.5 %shard_map.68 = (bf16[44,32,1792]{2,1,0:T(8,128)(2,1)S(1)}, f32[32,1792]{1,0:T(8,128)S(1)}, bf16[8,11,32,1024]{3,2,1,0:T(8,128)(2,1)S(1)}, f32[128,1792]{1,0:T(8,128)S(1)}) custom-call(bf16[44,224,1792]{2,1,0:T(8,128)(2,1)} %vv_hbm.1, bf16[44,32,1792]{2,1,0:T(8,128)(2,1)} %ov_hbm.1, bf16[44,32,256]{2,1,0:T(8,128)(2,1)} %oo_hbm.1, ...), custom_call_target="tpu_custom_call" | custom-call | tf_op jit(solution)/shard_map/pallas_call | solution.py:496
  138.2 2.4 %shard_map.69 = (bf16[44,32,1792]{2,1,0:T(8,128)(2,1)}, f32[32,1792]{1,0:T(8,128)}) custom-call(bf16[44,32,1792]{2,1,0:T(8,128)(2,1)S(1)} %get-tuple-element.6.dressed, f32[32,1792]{1,0:T(8,128)S(1)} %get-tuple-element.7.fock, bf16[8,11,32,1024]{3,2,1,0:T(8,128)(2,1)S(1)} %get-tuple-element.8.got, f32[128,1792]{1,0:T(8,128)S(1)} %get-tuple-element.9.occ_buf), custom_call_target="tpu_custom_call" | custom-call | tf_op jit(solution)/shard_map/pallas_call | solution.py:530
